TPU v7x, 512 devices: a whole 4x4x16 slice. The times are simulated.
512 devices in a mesh: dp: 16 (over x, z_hi, core), shard: 32 (over z_lo, y).
Axes of the slice: x: 4, y: 4, z: 16 (z_hi: 2, z_lo: 8; z = z_hi * 8 + z_lo), core: 2. Of those that a mesh axis runs over, the one named last changes fastest.
Arguments:
- tokens: bfloat16 [1024, 6144], P('dp', 'shard'), may hold values from -6 to 6
- cotangent: bfloat16 [1024, 6144], P('dp', 'shard'), may hold values from -12 to 12
- gate_proj: bfloat16 [2, 6144, 16384], P(None, 'dp', 'shard'), may hold values from -0.078125 to 0.078125
- up_proj: bfloat16 [2, 6144, 16384], P(None, 'dp', 'shard'), may hold values from -0.078125 to 0.078125
- down_proj: bfloat16 [2, 16384, 6144], P(None, 'shard', 'dp'), may hold values from -0.046875 to 0.046875
- slot_tokens: int32 [2, 256], P(None, 'dp'), may hold values from 0 to 63, as said below
- gate_weights: float32 [2, 256], P(None, 'dp'), may hold values from 0.1 to 1
- live_counts: int32 [2, 16], P(None, 'dp'), may hold values from 1 to 16, as said below
Outputs:
- grad_tokens: bfloat16 [1024, 6144], P('dp', 'shard')
- grad_gate_proj: bfloat16 [2, 6144, 16384], P(None, 'dp', 'shard')
- grad_up_proj: bfloat16 [2, 6144, 16384], P(None, 'dp', 'shard')
- grad_down_proj: bfloat16 [2, 16384, 6144], P(None, 'shard', 'dp')
Inputs may be any that keep to these rules, and one draw needn't show every extreme that they name: `slot_tokens`: for each expert and each index of dp, the 16 slots name 16 different tokens of that index. `live_counts`: the live slots of an expert at an index of dp are its first ones; 16 is reached at some index of every expert.
All inputs are finite; a program needn't handle non-finite values.
Results may differ from a plain program's by a relative error of at most 0.03.
Values may be sent and summed in bfloat16 or wider, within the bound.
No kernel may reach another device: no remote copies, remote signals or barrier semaphores. Data moves between devices by JAX's collectives and lax.ppermute only.
A program may use at most 64 MiB of HBM per device.

v0:
```python
import jax
import jax.numpy as jnp
from jax import lax
from jax.sharding import PartitionSpec as P


def gather_turned(arrays, axis, dims):
    turned = [jnp.moveaxis(a, dim, 0) for a, dim in zip(arrays, dims)]
    both = jnp.concatenate([t.reshape(len(t), -1) for t in turned], axis=1)
    result, at, outs = (lax.all_gather(both, axis, axis=0, tiled=True), 0, [])
    for t, dim in zip(turned, dims):
        slab = result[:, at : at + t[0].size].reshape(-1, *t.shape[1:])
        outs.append(jnp.moveaxis(slab, 0, dim))
        at += t[0].size
    return tuple(outs)


def in_one_piece(arrays, axis, split_dim, concat_dim, along):
    ends, at = ([], 0)
    for a in arrays[:-1]:
        at += a.shape[along]
        ends.append(at)
    both = jnp.concatenate(arrays, axis=along)
    return tuple(
        jnp.split(
            lax.all_to_all(both, axis, split_axis=split_dim, concat_axis=concat_dim, tiled=True),
            ends,
            axis=along,
        )
    )


def sent_together(arrays, axis, dim, along):
    ends, at = ([], 0)
    for a in arrays[:-1]:
        at += a.shape[along]
        ends.append(at)
    both = jnp.concatenate(arrays, axis=along)
    return tuple(
        jnp.split(lax.psum_scatter(both, axis, scatter_dimension=dim, tiled=True), ends, axis=along)
    )


def side_by_side(arrays, axis, dim, along):
    widths = [a.shape[along] for a in arrays]
    both = jnp.concatenate(arrays, axis=along)
    result = lax.all_gather(both, axis, axis=dim, tiled=True)
    return tuple(jnp.split(result, [sum(widths[:k]) for k in range(1, len(widths))], axis=along))


def cut_along(array, dim, count):
    before, after = (array.shape[:dim], array.shape[dim + 1 :])
    return jnp.moveaxis(array.reshape(*before, count, -1, *after), dim, 0)


def summed_on_arrival(array, axis, dim):
    count = lax.axis_size(axis)
    tiles = lax.all_to_all(cut_along(array, dim, count), axis, 0, 0, tiled=True)
    return jnp.sum(tiles.astype(jnp.float32), axis=0)


def slope_terms(gate_sum, up_sum, cot_hidden):
    sigmoid_part = jax.nn.sigmoid(gate_sum)
    grad_gate = (
        cot_hidden * up_sum * sigmoid_part * (1.0 + gate_sum * (1.0 - sigmoid_part))
    ).astype(jnp.bfloat16)
    grad_up = (cot_hidden * gate_sum * sigmoid_part).astype(jnp.bfloat16)
    return (grad_gate, grad_up)


def on_device(
    tokens, cotangent, gate_proj, up_proj, down_proj, slot_tokens, gate_weights, live_counts
):
    experts_here = slot_tokens.shape[0]
    slot_count = slot_tokens.shape[1]
    token_count = tokens.shape[0]
    position = lax.broadcasted_iota(jnp.int32, slot_tokens.shape, 1)
    alive_mask = (position < live_counts).astype(jnp.float32)
    picked = tokens[slot_tokens]
    weighted = (
        cotangent[slot_tokens].astype(jnp.float32) * (gate_weights * alive_mask)[:, :, None]
    ).astype(jnp.bfloat16)
    full_rows, full_cot = gather_turned((picked, weighted), "shard", (2, 2))
    spread = jnp.broadcast_to(live_counts[:, :, None], (experts_here, 1, lax.axis_size("dp")))
    block_rows, block_cot, heard = (
        *in_one_piece((full_rows, full_cot), "dp", 2, 1, 0),
        lax.all_to_all(spread, "dp", split_axis=2, concat_axis=1, tiled=True),
    )
    totals = jnp.sum(heard, axis=1).astype(jnp.float32)
    gate_part = jnp.einsum(
        "erd,edf->erf", block_rows, gate_proj, preferred_element_type=jnp.float32
    )
    up_part = jnp.einsum("erd,edf->erf", block_rows, up_proj, preferred_element_type=jnp.float32)
    cot_part = jnp.einsum("erd,efd->erf", block_cot, down_proj, preferred_element_type=jnp.float32)
    gate_sum, up_sum, cot_hidden = tuple(
        (
            part.astype(jnp.float32)
            for part in sent_together(
                (
                    gate_part.astype(jnp.bfloat16),
                    up_part.astype(jnp.bfloat16),
                    cot_part.astype(jnp.bfloat16),
                ),
                "dp",
                1,
                0,
            )
        )
    )
    hidden = (jax.nn.silu(gate_sum) * up_sum).astype(jnp.bfloat16)
    grad_gate, grad_up = slope_terms(gate_sum, up_sum, cot_hidden)
    hidden_all, gate_all, up_all = side_by_side((hidden, grad_gate, grad_up), "dp", 1, 0)
    scale_back = totals[:, :, None]
    grad_down_proj = (
        jnp.einsum("erf,erd->efd", hidden_all, block_cot, preferred_element_type=jnp.float32)
        / scale_back
    ).astype(jnp.bfloat16)
    grad_gate_proj = (
        jnp.einsum("erd,erf->edf", block_rows, gate_all, preferred_element_type=jnp.float32)
        / scale_back
    ).astype(jnp.bfloat16)
    grad_up_proj = (
        jnp.einsum("erd,erf->edf", block_rows, up_all, preferred_element_type=jnp.float32)
        / scale_back
    ).astype(jnp.bfloat16)
    back_term = (
        jnp.einsum("erf,edf->erd", gate_all, gate_proj, preferred_element_type=jnp.float32)
        + jnp.einsum("erf,edf->erd", up_all, up_proj, preferred_element_type=jnp.float32)
    ).astype(jnp.bfloat16)
    owned_rows = lax.all_to_all(back_term, "dp", split_axis=1, concat_axis=2, tiled=True)
    row_grads = summed_on_arrival(owned_rows.astype(jnp.float32).astype(jnp.bfloat16), "shard", 2)
    one_hot = (
        slot_tokens[:, :, None]
        == lax.broadcasted_iota(jnp.int32, (experts_here, slot_count, token_count), 2)
    ).astype(jnp.float32)
    grad_tokens = jnp.einsum("ert,erf->tf", one_hot, row_grads).astype(jnp.bfloat16)
    return (grad_tokens, grad_gate_proj, grad_up_proj, grad_down_proj)


def solution(mesh):
    in_specs = (
        P("dp", "shard"),
        P("dp", "shard"),
        P(None, "dp", "shard"),
        P(None, "dp", "shard"),
        P(None, "shard", "dp"),
        P(None, "dp"),
        P(None, "dp"),
        P(None, "dp"),
    )
    out_specs = (
        P("dp", "shard"),
        P(None, "dp", "shard"),
        P(None, "dp", "shard"),
        P(None, "shard", "dp"),
    )
    return jax.shard_map(
        on_device, mesh=mesh, in_specs=in_specs, out_specs=out_specs, check_vma=False
    )
```

profile of v0, /device:TPU:2, one launch (start us, length us, event | category | flops | bytes accessed | tf_op | source)
XLA Modules:
  0.0 493.9 jit_solution(5408034918978574355)
XLA Ops:
  7.2 0.0 copy-start
  7.2 0.0 reduce-scatter.2.cloned.1.call-start
  7.2 0.7 compare_select_fusion
  8.0 0.1 reshape.47
  8.1 1.4 gather_fusion.1
  9.4 1.4 gather_fusion
  10.8 0.8 compare_select_fusion.1
  11.6 0.1 fusion.14
  11.6 133.1 %all-gather = bf16[32,192,64]{1,2,0:T(8,128)(2,1)S(1)} all-gather(bf16[1,192,64]{1,2,0:T(8,128)(2,1)S(1)} %maximum_bitcast_fusion), channel_id=1, replica_groups=mesh['dp'=16,'shard'=32] {'shard'}, dimensions={0}, use_global_device_ids=true | all-gather | bytes 811008 | tf_op jit(solution)/shard_map/all_gather | solution.py:10
  144.7 0.6 copy.39
  145.3 1.1 reshape.67
  146.5 0.1 fusion.17
  146.5 0.1 pad_maximum_fusion.1
  146.6 6.2 %copy.40 = bf16[4,16,6144]{1,0,2:T(4,128)(2,1)} copy(bf16[4,16,6144]{2,1,0:T(8,128)(2,1)S(1)} %pad_maximum_fusion.1) | data formatting | bytes 1572864 | tf_op jit(solution)/shard_map/concatenate | solution.py:23
  152.8 9.3 %reshape.69 = bf16[16,2,12288]{2,1,0:T(2,128)(2,1)S(1)} reshape(bf16[6144,4,16]{2,1,0:T(4,128)(2,1)} %bitcast.53) | data formatting | bytes 1572864
  162.1 32.0 %all_to_all.44 = bf16[16,2,12288]{2,1,0:T(2,128)(2,1)S(1)} all-to-all(bf16[16,2,12288]{2,1,0:T(2,128)(2,1)S(1)} %reshape.69), channel_id=1, replica_groups=mesh['dp'=16,'shard'=32] {'dp'}, dimensions={0} | all-to-all | bytes 1572864 | tf_op jit(solution)/shard_map/all_to_all | solution.py:26
  194.1 5.6 %reshape.70 = bf16[6144,4,16]{2,1,0:T(4,128)(2,1)} reshape(bf16[16,2,12288]{2,1,0:T(2,128)(2,1)S(1)} %all_to_all.44) | data formatting | bytes 1572864
  199.8 6.6 %copy.53 = bf16[4,16,16,384]{3,2,1,0:T(8,128)(2,1)S(1)} copy(bf16[4,16,16,384]{1,0,3,2:T(4,128)(2,1)} %bitcast.54) | data formatting | bytes 1572864 | tf_op jit(solution)/shard_map/all_to_all | solution.py:26
  206.4 0.0 copy-start.2
  206.4 0.1 fusion.16
  206.5 0.1 copy.42
  206.5 0.9 copy-done.2
  207.5 0.4 convolution_convert_fusion.1
  207.9 0.0 copy-done
  207.9 0.0 copy-start.5
  207.9 0.4 convolution_convert_fusion.2
  208.4 0.1 copy.43
  208.5 0.0 copy-start.3
  208.5 0.7 copy-done.3
  209.2 0.0 copy-done.5
  209.2 0.5 convolution_convert_fusion
  209.7 1.3 pad_maximum_fusion
  211.0 0.0 reduce-scatter.2.cloned.1.call-update
  211.0 0.0 all-gather.3.cloned.1.call-start
  211.1 103.7 %reduce-scatter.2.cloned.1.call-done = bf16[6,16,512]{2,1,0:T(8,128)(2,1)} async-done(((bf16[6,256,512]{2,1,0:T(8,128)(2,1)}), bf16[6,16,512]{2,1,0:T(8,128)(2,1)}) %reduce-scatter.2.cloned.1.call-update) | async-done | bytes 98320 | tf_op jit(solution)/shard_map/reduce_scatter | solution.py:40
  314.8 0.8 fusion.4
  315.7 0.7 pad_maximum_fusion.2
  316.3 0.0 all-gather.3.cloned.1.call-update
  316.3 77.8 %all-gather.3.cloned.1.call-done = bf16[6,256,512]{2,1,0:T(8,128)(2,1)} async-done(((bf16[6,16,512]{2,1,0:T(8,128)(2,1)}), bf16[6,256,512]{2,1,0:T(8,128)(2,1)}) %all-gather.3.cloned.1.call-update) | async-done | bytes 1572880 | tf_op jit(solution)/shard_map/all_gather | solution.py:47
  394.2 0.0 copy-start.1
  394.2 1.6 fusion.18
  395.8 0.0 copy-done.1
  395.8 0.5 fusion
  396.3 0.0 copy-start.6
  396.3 0.4 copy.44
  396.7 20.0 %all_to_all.45 = bf16[2,256,384]{2,0,1:T(2,128)(2,1)S(1)} all-to-all(bf16[2,256,384]{2,0,1:T(2,128)(2,1)S(1)} %copy.44), channel_id=1, replica_groups=mesh['dp'=16,'shard'=32] {'dp'}, dimensions={1} | all-to-all | bytes 786432 | tf_op jit(solution)/shard_map/all_to_all | solution.py:130
  416.8 0.0 copy-done.6
  416.8 0.6 broadcast_in_dim.5
  417.4 6.1 %all-to-all-start.3 = ((s32[2,1,16]{0,1,2:T(1,128)}), s32[2,1,16]{0,1,2:T(1,128)S(1)}, u32[]{:S(2)}, u32[]{:S(2)}) async-start(s32[2,1,16]{0,1,2:T(1,128)} %broadcast_in_dim.5), calls=%async_computation.4 | async-start | bytes 16384 | tf_op jit(solution)/shard_map/all_to_all | solution.py:87
  423.5 0.9 copy.55
  424.3 1.3 reshape.44
  425.7 1.1 copy.46
  426.8 10.1 %all-to-all-done.3 = s32[2,1,16]{0,1,2:T(1,128)S(1)} async-done(((s32[2,1,16]{0,1,2:T(1,128)}), s32[2,1,16]{0,1,2:T(1,128)S(1)}, u32[]{:S(2)}, u32[]{:S(2)}) %all-to-all-start.3) | async-done | bytes 160 | tf_op jit(solution)/shard_map/all_to_all | solution.py:87
  436.9 19.6 %all-to-all-start.2 = ((bf16[32,2,16,192]{3,2,1,0:T(8,128)(2,1)}), bf16[32,2,16,192]{3,2,1,0:T(8,128)(2,1)S(1)}, u32[]{:S(2)}, u32[]{:S(2)}) async-start(bf16[32,2,16,192]{3,2,1,0:T(8,128)(2,1)} %copy.46), calls=%async_computation.3 | async-start | bytes 1048576 | tf_op jit(solution)/shard_map/all_to_all | solution.py:58
  456.5 1.3 divide_convert_fusion.1
  457.8 0.0 copy-start.4
  457.8 1.3 divide_convert_fusion.2
  459.1 0.0 copy-done.4
  459.1 0.0 copy-start.7
  459.1 1.4 divide_convert_fusion
  460.5 25.6 %all-to-all-done.2 = bf16[32,2,16,192]{3,2,1,0:T(8,128)(2,1)S(1)} async-done(((bf16[32,2,16,192]{3,2,1,0:T(8,128)(2,1)}), bf16[32,2,16,192]{3,2,1,0:T(8,128)(2,1)S(1)}, u32[]{:S(2)}, u32[]{:S(2)}) %all-to-all-start.2) | async-done | bytes 393248 | tf_op jit(solution)/shard_map/all_to_all | solution.py:58
  486.1 0.1 convert_reduce_fusion
  486.2 0.0 copy-done.7
  486.2 0.9 fusion.1
  (4 shorter events, 0.1 us)
Async XLA Ops:
  7.2 200.8 %copy-start = (bf16[2,384,512]{2,1,0:T(8,128)(2,1)S(1)}, bf16[2,384,512]{2,1,0:T(8,128)(2,1)}, u32[]{:S(2)}) copy-start(bf16[2,384,512]{2,1,0:T(8,128)(2,1)} %param.10) | copy-start | bytes 2359300
  7.2 307.6 %reduce-scatter.2.cloned.1.call-start = ((), (), s32[]{:S(2)}) async-start(), calls=%async_computation.5 | async-start | bytes 1671168 | tf_op jit(solution)/shard_map/reduce_scatter | solution.py:40
  206.4 1.1 copy-start.2
  207.9 1.3 copy-start.5
  208.5 0.7 copy-start.3
  211.0 183.1 %all-gather.3.cloned.1.call-start = ((), (), s32[]{:S(2)}) async-start(), calls=%async_computation.6 | async-start | bytes 1671168 | tf_op jit(solution)/shard_map/all_gather | solution.py:47
  394.2 1.6 copy-start.1
  396.3 20.5 %copy-start.6 = (s32[2,1]{0,1:T(1,128)S(1)}, s32[2,1]{0,1:T(1,128)}, u32[]{:S(2)}) copy-start(s32[2,1]{0,1:T(1,128)} %param.15) | copy-start | bytes 28
  417.4 19.5 %all-to-all-start.3 = ((s32[2,1,16]{0,1,2:T(1,128)}), s32[2,1,16]{0,1,2:T(1,128)S(1)}, u32[]{:S(2)}, u32[]{:S(2)}) async-start(s32[2,1,16]{0,1,2:T(1,128)} %broadcast_in_dim.5), calls=%async_computation.4 | async-start | bytes 16384 | tf_op jit(solution)/shard_map/all_to_all | solution.py:87
  436.9 49.2 %all-to-all-start.2 = ((bf16[32,2,16,192]{3,2,1,0:T(8,128)(2,1)}), bf16[32,2,16,192]{3,2,1,0:T(8,128)(2,1)S(1)}, u32[]{:S(2)}, u32[]{:S(2)}) async-start(bf16[32,2,16,192]{3,2,1,0:T(8,128)(2,1)} %copy.46), calls=%async_computation.3 | async-start | bytes 1048576 | tf_op jit(solution)/shard_map/all_to_all | solution.py:58
  457.8 1.3 copy-start.4
  459.1 27.1 %copy-start.7 = (s32[2,16]{1,0:T(2,128)S(1)}, s32[2,16]{1,0:T(2,128)}, u32[]{:S(2)}) copy-start(s32[2,16]{1,0:T(2,128)} %param.13) | copy-start | bytes 388
Sparse Core Ops, SparseCore 0:
  211.2 103.5 reduce-scatter.1
  318.7 75.3 all-gather.2
where the time goes:
time: 495 us; the launch traced here: 494 us
  waiting for transfers between devices  217 us (44%)
  blocking collectives  185 us (37%)
  local copies, waits for them, and re-layouts  38.6 us (8%)
  starting transfers between devices  25.7 us (5%)
  between operations  14.2 us (3%)
  matrix products  8.3 us (2%)
    all_gather x1, blocking collectives, gather_turned(): result, at, outs = (lax.all_gather(both, axis, axis=0, tiled=True), 0, [])  133 us
    reduce_scatter x1, waiting for transfers between devices, sent_together(): lax.psum_scatter(both, axis, scatter_dimension=dim, tiled=True)  104 us
    all_gather x1, waiting for transfers between devices, side_by_side(): result = lax.all_gather(both, axis, axis=dim, tiled=True)  77.8 us
    all_to_all x1, blocking collectives, in_one_piece(): lax.all_to_all(both, axis, split_axis=split_dim, concat_axis=concat_dim,...  32 us
    all_to_all x1, waiting for transfers between devices, summed_on_arrival(): tiles = lax.all_to_all(cut_along(array, dim, count), axis, 0, 0, tiled=True)  25.6 us
    all_to_all x1, blocking collectives, on_device(): lax.all_to_all(back_term, 'dp', split_axis=1, concat_axis=2, tiled=True)  20 us
    all_to_all x1, starting transfers between devices, summed_on_arrival(): tiles = lax.all_to_all(cut_along(array, dim, count), axis, 0, 0, tiled=True)  19.6 us
    unnamed x19, local copies, waits for them, and re-layouts  17.8 us
  transfers between devices with their start and end apart: 4, of which 4 were waited for; matrix products, arithmetic and copies ran while one was open for 1% of the time, Pallas kernels for 0%

commit v1 on v0

--- a/solution.py
+++ b/solution.py
@@ -7,7 +7,13 @@
 def gather_turned(arrays, axis, dims):
     turned = [jnp.moveaxis(a, dim, 0) for a, dim in zip(arrays, dims)]
     both = jnp.concatenate([t.reshape(len(t), -1) for t in turned], axis=1)
-    result, at, outs = (lax.all_gather(both, axis, axis=0, tiled=True), 0, [])
+    result, at, outs = (
+        jnp.concatenate(
+            lax.all_to_all(jnp.stack([both] * lax.axis_size(axis)), axis, 0, 0), axis=0
+        ),
+        0,
+        [],
+    )
     for t, dim in zip(turned, dims):
         slab = result[:, at : at + t[0].size].reshape(-1, *t.shape[1:])
         outs.append(jnp.moveaxis(slab, 0, dim))

time: 495 us -> 453 us (0.915)
  blocking collectives: 185 us -> 131 us
  waiting for transfers between devices: 217 us -> 229 us
    all_gather x1 -> x0, blocking collectives: 133 us -> none  [gather_turned(): result, at, outs = (lax.all_gather(both, axis, axis=0, tiled=True), 0, [])]
    all_to_all x0 -> x1, blocking collectives: none -> 67.2 us  [gather_turned(): lax.all_to_all(jnp.stack([both] * lax.axis_size(axis)), axis, 0, 0)]
    all_to_all x1, blocking collectives: 32 us -> 44 us  [in_one_piece(): lax.all_to_all(both, axis, split_axis=split_dim, concat_axis=concat_dim,...]
    reduce_scatter x1, waiting for transfers between devices: 104 us -> 116 us  [sent_together(): lax.psum_scatter(both, axis, scatter_dimension=dim, tiled=True)]
    unnamed x19 -> x18, local copies, waits for them, and re-layouts: 17.8 us -> 16.6 us
  transfers between devices with their start and end apart: 4 -> 4, of which waited for: 4 -> 4; matrix products, arithmetic and copies ran while one was open for 1% -> 2% of each run, Pallas kernels for 0% -> 0%
where the time goes in v1:
time: 453 us; the launch traced here: 452 us
  waiting for transfers between devices  229 us (51%)
  blocking collectives  131 us (29%)
  local copies, waits for them, and re-layouts  38.7 us (9%)
  starting transfers between devices  25.7 us (6%)
  between operations  14.3 us (3%)
  matrix products  8.32 us (2%)
  other arithmetic  4.63 us (1%)
    reduce_scatter x1, waiting for transfers between devices, sent_together(): lax.psum_scatter(both, axis, scatter_dimension=dim, tiled=True)  116 us
    all_gather x1, waiting for transfers between devices, side_by_side(): result = lax.all_gather(both, axis, axis=dim, tiled=True)  77.8 us
    all_to_all x1, blocking collectives, gather_turned(): lax.all_to_all(jnp.stack([both] * lax.axis_size(axis)), axis, 0, 0)  67.2 us
    all_to_all x1, blocking collectives, in_one_piece(): lax.all_to_all(both, axis, split_axis=split_dim, concat_axis=concat_dim,...  44 us
    all_to_all x1, waiting for transfers between devices, summed_on_arrival(): tiles = lax.all_to_all(cut_along(array, dim, count), axis, 0, 0, tiled=True)  25.6 us
    all_to_all x1, blocking collectives, on_device(): lax.all_to_all(back_term, 'dp', split_axis=1, concat_axis=2, tiled=True)  20 us
    all_to_all x1, starting transfers between devices, summed_on_arrival(): tiles = lax.all_to_all(cut_along(array, dim, count), axis, 0, 0, tiled=True)  19.6 us
    unnamed x18, local copies, waits for them, and re-layouts  16.6 us
  transfers between devices with their start and end apart: 4, of which 4 were waited for; matrix products, arithmetic and copies ran while one was open for 2% of the time, Pallas kernels for 0%

profile of v1, /device:TPU:2, one launch (start us, length us, event | category | flops | bytes accessed | tf_op | source)
XLA Modules:
  0.0 452.0 jit_solution(14560830559436735406)
XLA Ops:
  7.2 0.0 copy-start
  7.2 0.0 reduce-scatter.2.cloned.1.call-start
  7.2 0.7 compare_select_fusion
  8.0 0.1 reshape.53
  8.1 1.4 gather_fusion.1
  9.4 1.4 gather_fusion
  10.8 0.8 compare_select_fusion.1
  11.6 0.1 fusion.14
  11.6 0.1 stack.2
  11.8 67.2 %all_to_all.49 = bf16[32,192,64]{1,2,0:T(8,128)(2,1)S(1)} all-to-all(bf16[32,192,64]{1,2,0:T(8,128)(2,1)S(1)} %stack.2), channel_id=1, replica_groups=mesh['dp'=16,'shard'=32] {'shard'}, dimensions={0} | all-to-all | bytes 1572864 | tf_op jit(solution)/shard_map/all_to_all | solution.py:12
  79.0 0.6 copy.33
  79.6 1.1 reshape.47
  80.7 0.1 fusion.17
  80.8 0.1 pad_maximum_fusion.1
  80.9 6.2 %copy.34 = bf16[4,16,6144]{1,0,2:T(4,128)(2,1)} copy(bf16[4,16,6144]{2,1,0:T(8,128)(2,1)S(1)} %pad_maximum_fusion.1) | data formatting | bytes 1572864 | tf_op jit(solution)/shard_map/concatenate | solution.py:29
  87.1 9.3 %reshape.73 = bf16[16,2,12288]{2,1,0:T(2,128)(2,1)S(1)} reshape(bf16[6144,4,16]{2,1,0:T(4,128)(2,1)} %bitcast.51) | data formatting | bytes 1572864
  96.4 44.0 %all_to_all.50 = bf16[16,2,12288]{2,1,0:T(2,128)(2,1)S(1)} all-to-all(bf16[16,2,12288]{2,1,0:T(2,128)(2,1)S(1)} %reshape.73), channel_id=1, replica_groups=mesh['dp'=16,'shard'=32] {'dp'}, dimensions={0} | all-to-all | bytes 1572864 | tf_op jit(solution)/shard_map/all_to_all | solution.py:32
  140.4 5.6 %reshape.74 = bf16[6144,4,16]{2,1,0:T(4,128)(2,1)} reshape(bf16[16,2,12288]{2,1,0:T(2,128)(2,1)S(1)} %all_to_all.50) | data formatting | bytes 1572864
  146.0 6.6 %copy.47 = bf16[4,16,16,384]{3,2,1,0:T(8,128)(2,1)S(1)} copy(bf16[4,16,16,384]{1,0,3,2:T(4,128)(2,1)} %bitcast.52) | data formatting | bytes 1572864 | tf_op jit(solution)/shard_map/all_to_all | solution.py:32
  152.6 0.0 copy-start.2
  152.6 0.1 fusion.16
  152.7 0.1 copy.36
  152.8 0.9 copy-done.2
  153.7 0.4 convolution_convert_fusion.1
  154.2 0.0 copy-done
  154.2 0.0 copy-start.5
  154.2 0.4 convolution_convert_fusion.2
  154.6 0.1 copy.37
  154.7 0.0 copy-start.3
  154.7 0.7 copy-done.3
  155.4 0.0 copy-done.5
  155.4 0.5 convolution_convert_fusion
  155.9 1.3 pad_maximum_fusion
  157.3 0.0 reduce-scatter.2.cloned.1.call-update
  157.3 0.0 all-gather.2.cloned.1.call-start
  157.3 115.5 %reduce-scatter.2.cloned.1.call-done = bf16[6,16,512]{2,1,0:T(8,128)(2,1)} async-done(((bf16[6,256,512]{2,1,0:T(8,128)(2,1)}), bf16[6,16,512]{2,1,0:T(8,128)(2,1)}) %reduce-scatter.2.cloned.1.call-update) | async-done | bytes 98320 | tf_op jit(solution)/shard_map/reduce_scatter | solution.py:46
  272.9 0.8 fusion.4
  273.7 0.7 pad_maximum_fusion.2
  274.4 0.0 all-gather.2.cloned.1.call-update
  274.4 77.8 %all-gather.2.cloned.1.call-done = bf16[6,256,512]{2,1,0:T(8,128)(2,1)} async-done(((bf16[6,16,512]{2,1,0:T(8,128)(2,1)}), bf16[6,256,512]{2,1,0:T(8,128)(2,1)}) %all-gather.2.cloned.1.call-update) | async-done | bytes 1572880 | tf_op jit(solution)/shard_map/all_gather | solution.py:53
  352.2 0.0 copy-start.1
  352.2 1.6 fusion.18
  353.9 0.0 copy-done.1
  353.9 0.5 fusion
  354.3 0.0 copy-start.6
  354.4 0.4 copy.38
  354.8 20.0 %all_to_all.51 = bf16[2,256,384]{2,0,1:T(2,128)(2,1)S(1)} all-to-all(bf16[2,256,384]{2,0,1:T(2,128)(2,1)S(1)} %copy.38), channel_id=1, replica_groups=mesh['dp'=16,'shard'=32] {'dp'}, dimensions={1} | all-to-all | bytes 786432 | tf_op jit(solution)/shard_map/all_to_all | solution.py:136
  374.8 0.0 copy-done.6
  374.8 0.6 broadcast_in_dim.5
  375.4 6.1 %all-to-all-start.4 = ((s32[2,1,16]{0,1,2:T(1,128)}), s32[2,1,16]{0,1,2:T(1,128)S(1)}, u32[]{:S(2)}, u32[]{:S(2)}) async-start(s32[2,1,16]{0,1,2:T(1,128)} %broadcast_in_dim.5), calls=%async_computation.5 | async-start | bytes 16384 | tf_op jit(solution)/shard_map/all_to_all | solution.py:93
  381.5 0.9 copy.49
  382.4 1.3 reshape.50
  383.7 1.1 copy.40
  384.8 10.1 %all-to-all-done.4 = s32[2,1,16]{0,1,2:T(1,128)S(1)} async-done(((s32[2,1,16]{0,1,2:T(1,128)}), s32[2,1,16]{0,1,2:T(1,128)S(1)}, u32[]{:S(2)}, u32[]{:S(2)}) %all-to-all-start.4) | async-done | bytes 160 | tf_op jit(solution)/shard_map/all_to_all | solution.py:93
  394.9 19.6 %all-to-all-start.3 = ((bf16[32,2,16,192]{3,2,1,0:T(8,128)(2,1)}), bf16[32,2,16,192]{3,2,1,0:T(8,128)(2,1)S(1)}, u32[]{:S(2)}, u32[]{:S(2)}) async-start(bf16[32,2,16,192]{3,2,1,0:T(8,128)(2,1)} %copy.40), calls=%async_computation.4 | async-start | bytes 1048576 | tf_op jit(solution)/shard_map/all_to_all | solution.py:64
  414.5 1.3 divide_convert_fusion.1
  415.8 0.0 copy-start.4
  415.8 1.3 divide_convert_fusion.2
  417.1 0.0 copy-done.4
  417.1 1.4 divide_convert_fusion
  418.6 25.6 %all-to-all-done.3 = bf16[32,2,16,192]{3,2,1,0:T(8,128)(2,1)S(1)} async-done(((bf16[32,2,16,192]{3,2,1,0:T(8,128)(2,1)}), bf16[32,2,16,192]{3,2,1,0:T(8,128)(2,1)S(1)}, u32[]{:S(2)}, u32[]{:S(2)}) %all-to-all-start.3) | async-done | bytes 393248 | tf_op jit(solution)/shard_map/all_to_all | solution.py:64
  444.1 0.1 convert_reduce_fusion
  444.2 0.0 copy-done.7
  444.2 0.9 fusion.1
  (5 shorter events, 0.1 us)
Async XLA Ops:
  7.2 147.0 %copy-start = (bf16[2,384,512]{2,1,0:T(8,128)(2,1)S(1)}, bf16[2,384,512]{2,1,0:T(8,128)(2,1)}, u32[]{:S(2)}) copy-start(bf16[2,384,512]{2,1,0:T(8,128)(2,1)} %param.10) | copy-start | bytes 2359300
  7.2 265.7 %reduce-scatter.2.cloned.1.call-start = ((), (), s32[]{:S(2)}) async-start(), calls=%async_computation.6 | async-start | bytes 1671168 | tf_op jit(solution)/shard_map/reduce_scatter | solution.py:46
  152.6 1.1 copy-start.2
  154.2 1.3 copy-start.5
  154.7 0.7 copy-start.3
  157.3 194.9 %all-gather.2.cloned.1.call-start = ((), (), s32[]{:S(2)}) async-start(), calls=%async_computation.7 | async-start | bytes 1671168 | tf_op jit(solution)/shard_map/all_gather | solution.py:53
  352.2 1.6 copy-start.1
  354.3 20.5 %copy-start.6 = (s32[2,1]{0,1:T(1,128)S(1)}, s32[2,1]{0,1:T(1,128)}, u32[]{:S(2)}) copy-start(s32[2,1]{0,1:T(1,128)} %param.15) | copy-start | bytes 28
  375.4 19.5 %all-to-all-start.4 = ((s32[2,1,16]{0,1,2:T(1,128)}), s32[2,1,16]{0,1,2:T(1,128)S(1)}, u32[]{:S(2)}, u32[]{:S(2)}) async-start(s32[2,1,16]{0,1,2:T(1,128)} %broadcast_in_dim.5), calls=%async_computation.5 | async-start | bytes 16384 | tf_op jit(solution)/shard_map/all_to_all | solution.py:93
  394.9 49.2 %all-to-all-start.3 = ((bf16[32,2,16,192]{3,2,1,0:T(8,128)(2,1)}), bf16[32,2,16,192]{3,2,1,0:T(8,128)(2,1)S(1)}, u32[]{:S(2)}, u32[]{:S(2)}) async-start(bf16[32,2,16,192]{3,2,1,0:T(8,128)(2,1)} %copy.40), calls=%async_computation.4 | async-start | bytes 1048576 | tf_op jit(solution)/shard_map/all_to_all | solution.py:64
  415.8 1.3 copy-start.4
  417.1 27.1 %copy-start.7 = (s32[2,16]{1,0:T(2,128)S(1)}, s32[2,16]{1,0:T(2,128)}, u32[]{:S(2)}) copy-start(s32[2,16]{1,0:T(2,128)} %param.13) | copy-start | bytes 388
Sparse Core Ops, SparseCore 0:
  157.4 115.4 reduce-scatter.1
  276.8 75.3 all-gather.1
